TPU v7x, 256 devices: a whole 4x4x8 slice. The times are simulated.
256 devices in a mesh: bev: 64 (over z, x, core), scene: 4 (over y).
Axes of the slice: x: 4, y: 4, z: 8, core: 2. Of those that a mesh axis runs over, the one named last changes fastest.
Arguments:
- context: bfloat16 [4, 80, 16384], P('scene', None, 'bev'), may hold values from -24 to 24
- depth_logits: float32 [4, 112, 16384], P('scene', None, 'bev'), may hold values from -20 to 300
- send_count: int32 [4, 64, 64], P('scene', 'bev'), may hold values from 0 to 1024, as said below
- slot_point: int32 [4, 64, 64, 1024], P('scene', 'bev'), may hold values from 0 to 28671, as said below
- slot_cell: int32 [4, 64, 64, 1024], P('scene', 'bev'), may hold values from 0 to 255
Outputs:
- bev_features: bfloat16 [16384, 320], P(('bev', 'scene'))
Inputs may be any that keep to these rules, and one draw needn't show every extreme that they name: `send_count`: one entry is 1024 in every pixel block's row. `slot_point`: the live slots of one pixel block name distinct points; slots at or past the count are unused.
All inputs are finite; a program needn't handle non-finite values.
Results may differ from a plain program's by a relative error of at most 0.0062.
Values may be sent and summed in bfloat16 or wider, within the bound.
No kernel may reach another device: no remote copies, remote signals or barrier semaphores. Data moves between devices by JAX's collectives and lax.ppermute only.
A program may use at most 128 MiB of HBM per device.

v0:
```python
import jax
import jax.numpy as jnp
from jax import lax
from jax.sharding import PartitionSpec as P

GRID = 128


def in_blocks(x, dim, devices):
    before, after = (x.shape[:dim], x.shape[dim + 1 :])
    return jnp.moveaxis(x.reshape(*before, devices, -1, *after), dim, 0)


def sum_at_owner(x, axis, dim):
    devices = lax.axis_size(axis)
    tiles = lax.all_to_all(in_blocks(x, dim, devices), axis, 0, 0, tiled=True)
    return jnp.sum(tiles.astype(jnp.float32), axis=0)


def pool_each(values, cell_ids, strip_cells):
    onehot = (
        cell_ids[:, :, None] == jnp.arange(strip_cells, dtype=jnp.int32)[None, None, :]
    ).astype(jnp.bfloat16)
    return jnp.einsum("gcs,gsn->gnc", values, onehot, preferred_element_type=jnp.float32)


def select_points(point_ids, context_map, depth_prob):
    pix_block = context_map.shape[1]
    depth_bins = depth_prob.shape[0]
    depth_bin = point_ids // pix_block
    pixel_ids = point_ids % pix_block
    pixel_hot = (
        pixel_ids[:, :, None] == jnp.arange(pix_block, dtype=jnp.int32)[None, None, :]
    ).astype(jnp.bfloat16)
    depth_hot = (
        depth_bin[:, :, None] == jnp.arange(depth_bins, dtype=jnp.int32)[None, None, :]
    ).astype(jnp.bfloat16)
    features = jnp.einsum("nsp,cp->ncs", pixel_hot, context_map, preferred_element_type=jnp.float32)
    prob_rows = jnp.einsum("nsk,kp->nsp", depth_hot, depth_prob, preferred_element_type=jnp.float32)
    weight = jnp.sum(prob_rows * pixel_hot.astype(jnp.float32), axis=2)
    return (features * weight[:, None, :]).astype(jnp.bfloat16)


def body(context, depth_logits, send_count, slot_point, slot_cell):
    strips = lax.axis_size("bev")
    scenes = lax.axis_size("scene")
    strip_cells = GRID * GRID // strips
    channels = context.shape[1]
    capacity = slot_point.shape[3]
    depth_prob = jax.nn.softmax(depth_logits[0], axis=0).astype(jnp.bfloat16)
    context_map = context[0]
    counts = send_count[0, 0]
    points = slot_point[0, 0]
    live_mask = jnp.arange(capacity, dtype=jnp.int32)[None, :] < counts[:, None]
    targets = jnp.where(live_mask, slot_cell[0, 0], strip_cells)
    values = select_points(points, context_map, depth_prob)
    strip_sum = sum_at_owner(
        pool_each(values, targets, strip_cells)
        .reshape(strip_cells * lax.axis_size("bev"), channels)
        .astype(jnp.bfloat16),
        "bev",
        0,
    )
    quarter = strip_cells // scenes
    rounded = strip_sum.astype(jnp.bfloat16).reshape(scenes, quarter, 1, channels)
    moved = lax.all_to_all(rounded, "scene", split_axis=0, concat_axis=2, tiled=True)
    return moved.reshape(quarter, scenes * channels)


def solution(mesh):
    return jax.shard_map(
        body,
        mesh=mesh,
        in_specs=(
            P("scene", None, "bev"),
            P("scene", None, "bev"),
            P("scene", "bev", None),
            P("scene", "bev", None, None),
            P("scene", "bev", None, None),
        ),
        out_specs=P(("bev", "scene"), None),
        check_vma=False,
    )
```

profile of v0, /device:TPU:2, one launch (start us, length us, event | category | flops | bytes accessed | tf_op | source)
XLA Modules:
  0.0 141.6 jit_solution(11307070710234492354)
XLA Ops:
  0.0 0.0 copy-start
  0.0 0.9 reduce_max.9
  0.9 0.9 fusion.13
  1.9 1.3 add_select_fusion
  3.2 19.7 %multiply_reduce_fusion = f32[64,1024]{1,0:T(8,128)S(1)} fusion(s32[64,1024]{1,0:T(8,128)S(1)} %get-tuple-element.6, s32[64,1024]{1,0:T(8,128)S(1)} %get-tuple-element.5, f32[1,112,256]{2,1,0:T(8,128)} %param.6, f32[256]{0:T(256)S(1)} %fusion.13, f32[256]{0:T(256)S(1)} %reduce_max.9), kind=kOutput, calls=%fused_computation | convolution fusion | flops 3849342976 | bytes 903168 | tf_op jit(solution)/shard_map/nsk,kp->nsp/dot_general | solution.py:39
  22.9 0.0 copy-done
  22.9 15.2 %multiply_convert_fusion.7 = bf16[64,1024,80]{1,2,0:T(8,128)(2,1)S(1)} fusion(f32[64,1024]{1,0:T(8,128)S(1)} %multiply_reduce_fusion, s32[64,1024]{1,0:T(8,128)S(1)} %get-tuple-element.6, bf16[1,80,256]{2,1,0:T(8,128)(2,1)S(1)} %copy-done), kind=kOutput, calls=%fused_computation.10.clone.clone.clone.clone.2 | convolution fusion | flops 2711617536 | bytes 11051008 | tf_op jit(solution)/shard_map/nsp,cp->ncs/dot_general | solution.py:38
  38.1 18.1 %fusion.8 = bf16[64,256,80]{1,2,0:T(8,128)(2,1)S(1)} fusion(s32[64,1024]{1,0:T(8,128)S(1)} %get-tuple-element.7, bf16[64,1024,80]{1,2,0:T(8,128)(2,1)S(1)} %multiply_convert_fusion.7), kind=kOutput, calls=%fused_computation.13 | convolution fusion | flops 2702442496 | bytes 13369344 | tf_op jit(solution)/shard_map/gcs,gsn->gnc/dot_general | solution.py:24
  56.2 74.3 %all_to_all.20 = bf16[64,256,80]{1,2,0:T(8,128)(2,1)S(1)} all-to-all(bf16[64,256,80]{1,2,0:T(8,128)(2,1)S(1)} %fusion.8), channel_id=1, replica_groups=mesh['bev'=64,'scene'=4] {'bev'}, dimensions={0} | all-to-all | bytes 5242880 | tf_op jit(solution)/shard_map/all_to_all | solution.py:16
  130.4 0.4 reduce_sum.32
  130.8 0.1 copy.9
  130.9 9.9 %all_to_all.21 = bf16[4,64,1,80]{3,1,2,0:T(8,128)(2,1)S(1)} all-to-all(bf16[4,64,1,80]{3,1,2,0:T(8,128)(2,1)S(1)} %bitcast.62), channel_id=1, replica_groups=mesh['bev'=64,'scene'=4] {'scene'}, dimensions={0} | all-to-all | bytes 81920 | tf_op jit(solution)/shard_map/all_to_all | solution.py:66
  140.8 0.1 copy.11
  140.9 0.7 reshape.91
Async XLA Ops:
  0.0 22.9 %copy-start = (bf16[1,80,256]{2,1,0:T(8,128)(2,1)S(1)}, bf16[1,80,256]{2,1,0:T(8,128)(2,1)}, u32[]{:S(2)}) copy-start(bf16[1,80,256]{2,1,0:T(8,128)(2,1)} %param.5) | copy-start | bytes 122884
where the time goes:
time: 142 us
  blocking collectives  84.2 us (59%)
  matrix products  53 us (37%)
  other arithmetic  3.52 us (2%)
    all_to_all x1, blocking collectives, sum_at_owner(): tiles = lax.all_to_all(in_blocks(x, dim, devices), axis, 0, 0, tiled=True)  74.3 us
    dot_general x1, matrix products, select_points(): jnp.einsum('nsk,kp->nsp', depth_hot, depth_prob, preferred_element_type=j...  19.7 us
    dot_general x1, matrix products, pool_each(): jnp.einsum('gcs,gsn->gnc', values, onehot, preferred_element_type=jnp.flo...  18.1 us
    dot_general x1, matrix products, select_points(): jnp.einsum('nsp,cp->ncs', pixel_hot, context_map, preferred_element_type=...  15.2 us
    all_to_all x1, blocking collectives, body(): lax.all_to_all(rounded, 'scene', split_axis=0, concat_axis=2, tiled=True)  9.88 us

commit v1 on v0

--- a/solution.py
+++ b/solution.py
@@ -4,6 +4,18 @@
 from jax.sharding import PartitionSpec as P
 
 GRID = 128
+
+
+def exchange_directly(x, axis, split, join):
+    ways, here = (lax.axis_size(axis), lax.axis_index(axis))
+    width = x.shape[split] // ways
+    turned = jnp.roll(x, -here * width, axis=split)
+    got = [lax.slice_in_dim(turned, 0, width, axis=split)]
+    for far in range(1, ways):
+        sent = lax.slice_in_dim(turned, far * width, (far + 1) * width, axis=split)
+        got.append(lax.ppermute(sent, axis, [(d, (d + far) % ways) for d in range(ways)]))
+    line = jnp.concatenate(got[::-1], axis=join)
+    return jnp.roll(line, (here + 1) * got[0].shape[join], axis=join)
 
 
 def in_blocks(x, dim, devices):
@@ -63,7 +75,7 @@
     )
     quarter = strip_cells // scenes
     rounded = strip_sum.astype(jnp.bfloat16).reshape(scenes, quarter, 1, channels)
-    moved = lax.all_to_all(rounded, "scene", split_axis=0, concat_axis=2, tiled=True)
+    moved = exchange_directly(rounded, "scene", 0, 2)
     return moved.reshape(quarter, scenes * channels)
 
 

time: 142 us -> 142 us (level)
  blocking collectives: 84.2 us -> 0 us
  waiting for transfers between devices: 0 us -> 65.5 us
  starting transfers between devices: 0 us -> 17.3 us
    all_to_all x2 -> x0, blocking collectives: 84.2 us -> none  [the longest x1 74.3 us: sum_at_owner(): tiles = lax.all_to_all(in_blocks(x, dim, devices), axis, 0, 0, tiled=True)]
    all_to_all x0 -> x1, waiting for transfers between devices: none -> 62.4 us  [sum_at_owner(): tiles = lax.all_to_all(in_blocks(x, dim, devices), axis, 0, 0, tiled=True)]
    all_to_all x0 -> x1, starting transfers between devices: none -> 12 us  [sum_at_owner(): tiles = lax.all_to_all(in_blocks(x, dim, devices), axis, 0, 0, tiled=True)]
    ppermute x0 -> x3, starting transfers between devices: none -> 5.3 us  [exchange_directly(): lax.ppermute(sent, axis, [(d, (d + far) % ways) for d in range(ways)])]
    ppermute x0 -> x3, waiting for transfers between devices: none -> 3.04 us  [exchange_directly(): lax.ppermute(sent, axis, [(d, (d + far) % ways) for d in range(ways)])]
  transfers between devices with their start and end apart: 0 -> 4, of which waited for: 0 -> 2; matrix products, arithmetic and copies ran while one was open for 0% -> 0% of each run, Pallas kernels for 0% -> 0%
where the time goes in v1:
time: 142 us; the launch traced here: 141 us
  waiting for transfers between devices  65.5 us (46%)
  matrix products  53.8 us (38%)
  starting transfers between devices  17.3 us (12%)
  other arithmetic  3.57 us (3%)
    all_to_all x1, waiting for transfers between devices, sum_at_owner(): tiles = lax.all_to_all(in_blocks(x, dim, devices), axis, 0, 0, tiled=True)  62.4 us
    dot_general x1, matrix products, select_points(): jnp.einsum('nsk,kp->nsp', depth_hot, depth_prob, preferred_element_type=j...  19.8 us
    dot_general x1, matrix products, pool_each(): jnp.einsum('gcs,gsn->gnc', values, onehot, preferred_element_type=jnp.flo...  18.9 us
    dot_general x1, matrix products, select_points(): jnp.einsum('nsp,cp->ncs', pixel_hot, context_map, preferred_element_type=...  15.2 us
    all_to_all x1, starting transfers between devices, sum_at_owner(): tiles = lax.all_to_all(in_blocks(x, dim, devices), axis, 0, 0, tiled=True)  12 us
    ppermute x3, starting transfers between devices, exchange_directly(): lax.ppermute(sent, axis, [(d, (d + far) % ways) for d in range(ways)])  5.3 us
    ppermute x3, waiting for transfers between devices, exchange_directly(): lax.ppermute(sent, axis, [(d, (d + far) % ways) for d in range(ways)])  3.04 us
  transfers between devices with their start and end apart: 4, of which 2 were waited for; matrix products, arithmetic and copies ran while one was open for 0% of the time, Pallas kernels for 0%

profile of v1, /device:TPU:2, one launch (start us, length us, event | category | flops | bytes accessed | tf_op | source)
XLA Modules:
  0.0 141.3 jit_solution(212688974850071946)
XLA Ops:
  0.0 0.0 copy-start
  0.0 0.9 reduce_max.9
  0.9 0.9 fusion.13
  1.9 1.3 add_select_fusion
  3.2 19.8 %multiply_reduce_fusion = f32[64,1024]{1,0:T(8,128)S(1)} fusion(s32[64,1024]{1,0:T(8,128)S(1)} %get-tuple-element.6, s32[64,1024]{1,0:T(8,128)S(1)} %get-tuple-element.5, f32[1,112,256]{2,1,0:T(8,128)} %param.6, f32[256]{0:T(256)S(1)} %fusion.13, f32[256]{0:T(256)S(1)} %reduce_max.9), kind=kOutput, calls=%fused_computation | convolution fusion | flops 3849342976 | bytes 903168 | tf_op jit(solution)/shard_map/nsk,kp->nsp/dot_general | solution.py:51
  22.9 0.0 copy-done
  22.9 15.2 %multiply_convert_fusion.7 = bf16[64,1024,80]{1,2,0:T(8,128)(2,1)S(1)} fusion(f32[64,1024]{1,0:T(8,128)S(1)} %multiply_reduce_fusion, s32[64,1024]{1,0:T(8,128)S(1)} %get-tuple-element.6, bf16[1,80,256]{2,1,0:T(8,128)(2,1)S(1)} %copy-done), kind=kOutput, calls=%fused_computation.10.clone.clone.clone.clone.2 | convolution fusion | flops 2711617536 | bytes 11051008 | tf_op jit(solution)/shard_map/nsp,cp->ncs/dot_general | solution.py:50
  38.1 18.9 %fusion.8 = bf16[64,256,80]{1,2,0:T(8,128)(2,1)} fusion(s32[64,1024]{1,0:T(8,128)S(1)} %get-tuple-element.10, bf16[64,1024,80]{1,2,0:T(8,128)(2,1)S(1)} %multiply_convert_fusion.7), kind=kOutput, calls=%fused_computation.13 | convolution fusion | flops 2702442496 | bytes 13369344 | tf_op jit(solution)/shard_map/gcs,gsn->gnc/dot_general | solution.py:36
  57.0 12.0 %all-to-all-start = ((bf16[64,256,80]{1,2,0:T(8,128)(2,1)}), bf16[64,256,80]{1,2,0:T(8,128)(2,1)S(1)}, u32[]{:S(2)}, u32[]{:S(2)}) async-start(bf16[64,256,80]{1,2,0:T(8,128)(2,1)} %fusion.8), calls=%async_computation | async-start | bytes 5242880 | tf_op jit(solution)/shard_map/all_to_all | solution.py:28
  69.0 62.4 %all-to-all-done = bf16[64,256,80]{1,2,0:T(8,128)(2,1)S(1)} async-done(((bf16[64,256,80]{1,2,0:T(8,128)(2,1)}), bf16[64,256,80]{1,2,0:T(8,128)(2,1)S(1)}, u32[]{:S(2)}, u32[]{:S(2)}) %all-to-all-start) | async-done | bytes 2621472 | tf_op jit(solution)/shard_map/all_to_all | solution.py:28
  131.5 0.4 reduce_sum.32
  131.9 0.1 copy.9
  132.0 0.1 fusion.14
  132.1 3.1 %collective-permute-start = (bf16[1,64,1,80]{3,1,0,2:T(8,128)(2,1)S(1)}, bf16[1,64,1,80]{3,1,0,2:T(8,128)(2,1)S(1)}, u32[]{:S(2)}, u32[]{:S(2)}) collective-permute-start(bf16[1,64,1,80]{3,1,0,2:T(8,128)(2,1)S(1)} %get-tuple-element.9), channel_id=1, source_target_pairs={{0,3},{1,0},{2,1},{3,2},{4,7},{5,4},{6,5},{7,6},{8,11},{9,8},{10,9... | collective-permute-start | bytes 30728 | tf_op jit(solution)/shard_map/ppermute | solution.py:16
  135.2 0.0 collective-permute-start.2
  135.2 2.2 %collective-permute-start.1 = (bf16[1,64,1,80]{3,1,0,2:T(8,128)(2,1)S(1)}, bf16[1,64,1,80]{3,1,0,2:T(8,128)(2,1)S(1)}, u32[]{:S(2)}, u32[]{:S(2)}) collective-permute-start(bf16[1,64,1,80]{3,1,0,2:T(8,128)(2,1)S(1)} %get-tuple-element.8), channel_id=1, source_target_pairs={{0,2},{1,3},{2,0},{3,1},{4,6},{5,7},{6,4},{7,5},{8,10},{9,11},{10,... | collective-permute-start | bytes 30728 | tf_op jit(solution)/shard_map/ppermute | solution.py:16
  137.4 0.0 collective-permute-done
  137.4 3.0 %collective-permute-done.1 = bf16[1,64,1,80]{3,1,0,2:T(8,128)(2,1)S(1)} collective-permute-done((bf16[1,64,1,80]{3,1,0,2:T(8,128)(2,1)S(1)}, bf16[1,64,1,80]{3,1,0,2:T(8,128)(2,1)S(1)}, u32[]{:S(2)}, u32[]{:S(2)}) %collective-permute-start.1) | collective-permute-done | bytes 10272 | tf_op jit(solution)/shard_map/ppermute | solution.py:16
  140.4 0.0 collective-permute-done.2
  140.5 0.1 copy.10
  140.6 0.7 reshape.90
  (10 shorter events, 0.1 us)
Async XLA Ops:
  0.0 22.9 %copy-start = (bf16[1,80,256]{2,1,0:T(8,128)(2,1)S(1)}, bf16[1,80,256]{2,1,0:T(8,128)(2,1)}, u32[]{:S(2)}) copy-start(bf16[1,80,256]{2,1,0:T(8,128)(2,1)} %param.5) | copy-start | bytes 122884
  57.0 74.5 %all-to-all-start = ((bf16[64,256,80]{1,2,0:T(8,128)(2,1)}), bf16[64,256,80]{1,2,0:T(8,128)(2,1)S(1)}, u32[]{:S(2)}, u32[]{:S(2)}) async-start(bf16[64,256,80]{1,2,0:T(8,128)(2,1)} %fusion.8), calls=%async_computation | async-start | bytes 5242880 | tf_op jit(solution)/shard_map/all_to_all | solution.py:28
  132.1 5.3 %collective-permute-start = (bf16[1,64,1,80]{3,1,0,2:T(8,128)(2,1)S(1)}, bf16[1,64,1,80]{3,1,0,2:T(8,128)(2,1)S(1)}, u32[]{:S(2)}, u32[]{:S(2)}) collective-permute-start(bf16[1,64,1,80]{3,1,0,2:T(8,128)(2,1)S(1)} %get-tuple-element.9), channel_id=1, source_target_pairs={{0,3},{1,0},{2,1},{3,2},{4,7},{5,4},{6,5},{7,6},{8,11},{9,8},{10,9... | collective-permute-start | bytes 30728 | tf_op jit(solution)/shard_map/ppermute | solution.py:16
  135.2 5.3 %collective-permute-start.2 = (bf16[1,64,1,80]{3,1,0,2:T(8,128)(2,1)S(1)}, bf16[1,64,1,80]{3,1,0,2:T(8,128)(2,1)S(1)}, u32[]{:S(2)}, u32[]{:S(2)}) collective-permute-start(bf16[1,64,1,80]{3,1,0,2:T(8,128)(2,1)S(1)} %get-tuple-element.7), channel_id=1, source_target_pairs={{0,1},{1,2},{2,3},{3,0},{4,5},{5,6},{6,7},{7,4},{8,9},{9,10},{10,1... | collective-permute-start | bytes 30728 | tf_op jit(solution)/shard_map/ppermute | solution.py:16
  135.2 5.2 %collective-permute-start.1 = (bf16[1,64,1,80]{3,1,0,2:T(8,128)(2,1)S(1)}, bf16[1,64,1,80]{3,1,0,2:T(8,128)(2,1)S(1)}, u32[]{:S(2)}, u32[]{:S(2)}) collective-permute-start(bf16[1,64,1,80]{3,1,0,2:T(8,128)(2,1)S(1)} %get-tuple-element.8), channel_id=1, source_target_pairs={{0,2},{1,3},{2,0},{3,1},{4,6},{5,7},{6,4},{7,5},{8,10},{9,11},{10,... | collective-permute-start | bytes 30728 | tf_op jit(solution)/shard_map/ppermute | solution.py:16
